TPU v7x, 32 devices: a 4x4x1 block of a 4x4x8 slice. The times are simulated.
32 devices in a mesh: dp: 1 (over z), tx: 4 (over y), ty: 8 (over x, core).
Axes of the slice: x: 4, y: 4, z: 1, core: 2. Of those that a mesh axis runs over, the one named last changes fastest.
The devices are a block of a 4x4x8 slice.
Arguments:
- x: bfloat16 [4096, 2048], P('dp', ('tx', 'ty'))
- seg_ids: int32 [4096], P('dp')
- positions: int32 [4096], P('dp')
- ln1_gain: bfloat16 [2, 2048], P(None, ('tx', 'ty'))
- ln1_bias: bfloat16 [2, 2048], P(None, ('tx', 'ty'))
- w_q: bfloat16 [2, 2048, 16, 128], P(None, 'tx', 'ty')
- b_q: bfloat16 [2, 16, 128], P(None, 'ty')
- w_k: bfloat16 [2, 2048, 16, 128], P(None, 'tx', 'ty')
- b_k: bfloat16 [2, 16, 128], P(None, 'ty')
- w_v: bfloat16 [2, 2048, 16, 128], P(None, 'tx', 'ty')
- b_v: bfloat16 [2, 16, 128], P(None, 'ty')
- w_o: bfloat16 [2, 16, 128, 2048], P(None, 'ty', None, 'tx')
- b_o: bfloat16 [2, 2048], P(None, ('tx', 'ty'))
- ln2_gain: bfloat16 [2, 2048], P(None, ('tx', 'ty'))
- ln2_bias: bfloat16 [2, 2048], P(None, ('tx', 'ty'))
- w_up: bfloat16 [2, 2048, 8192], P(None, 'tx', 'ty')
- b_up: bfloat16 [2, 8192], P(None, ('ty', 'tx'))
- w_down: bfloat16 [2, 8192, 2048], P(None, 'ty', 'tx')
- b_down: bfloat16 [2, 2048], P(None, ('tx', 'ty'))
Outputs:
- output 1: bfloat16 [4096, 2048], P('dp', ('tx', 'ty'))
- output 2: bfloat16 [2, 4096, 16, 128], P(None, ('dp', 'tx'), 'ty')
- output 3: bfloat16 [2, 4096, 16, 128], P(None, ('dp', 'tx'), 'ty')
All inputs are finite; a program needn't handle non-finite values.
Results may differ from a plain program's by a relative error of at most 0.0119909.
Values are sent between devices in bfloat16 or wider.
A program may use at most 768 MiB of HBM per device.

v0:
```python
import math
import jax
import jax.numpy as jnp
from jax import lax
from jax.sharding import PartitionSpec as P

WINDOW = 4096
ROPE_THETA = 100000.0


def rotary_tables(positions, head_dim):
    half_dim = head_dim // 2
    inv_freq = jnp.exp(jnp.arange(half_dim, dtype=jnp.float32) * (-2.0 * math.log(ROPE_THETA) / head_dim))
    angles = positions.astype(jnp.float32)[:, None] * inv_freq[None, :]
    return jnp.cos(angles)[:, None, :], jnp.sin(angles)[:, None, :]


def rotary(head_vals, cos_t, sin_t):
    half_dim = head_vals.shape[-1] // 2
    first_half = head_vals[..., :half_dim]
    second_half = head_vals[..., half_dim:]
    return jnp.concatenate([first_half * cos_t - second_half * sin_t, second_half * cos_t + first_half * sin_t], axis=-1)


def norm_sharded(x_loc, gain, bias, d_model):
    x_f32 = x_loc.astype(jnp.float32)
    local_sums = jnp.stack([jnp.sum(x_f32, axis=-1), jnp.sum(x_f32 * x_f32, axis=-1)])
    norm_sums = lax.psum(local_sums, ('tx', 'ty'))
    row_mean = norm_sums[0] / d_model
    row_var = norm_sums[1] / d_model - row_mean * row_mean
    normed = (x_f32 - row_mean[:, None]) * lax.rsqrt(row_var + 1e-5)[:, None]
    return (normed * gain.astype(jnp.float32) + bias.astype(jnp.float32)).astype(jnp.bfloat16)


def local_attention(q_loc, key_rows, val_rows, seg_q, seg_k, q_start):
    n_query, loc_heads, head_dim = q_loc.shape
    n_key, kv_loc = key_rows.shape[0], key_rows.shape[1]
    group_size = loc_heads // kv_loc
    q_block = min(n_query, 128)
    key_len = min(n_key, WINDOW + q_block)
    n_blocks = n_query // q_block
    score_scale = head_dim ** -0.5
    q_blocks = q_loc.reshape(n_blocks, q_block, kv_loc, group_size, head_dim)
    seg_blocks = seg_q.reshape(n_blocks, q_block)

    def one_block(block_args):
        blk_idx, q_blk, seg_qb = block_args
        q_first = q_start + blk_idx * q_block
        k_first = jnp.clip(q_first + q_block - key_len, 0, n_key - key_len)
        k_blk = lax.dynamic_slice_in_dim(key_rows, k_first, key_len, 0)
        v_blk = lax.dynamic_slice_in_dim(val_rows, k_first, key_len, 0)
        seg_kb = lax.dynamic_slice_in_dim(seg_k, k_first, key_len, 0)
        scores = jnp.einsum('qkgd,skd->kgqs', q_blk, k_blk, preferred_element_type=jnp.float32) * score_scale
        key_gap = (q_first + jnp.arange(q_block))[:, None] - (k_first + jnp.arange(key_len))[None, :]
        allowed = (key_gap >= 0) & (key_gap < WINDOW) & (seg_qb[:, None] == seg_kb[None, :])
        scores = jnp.where(allowed, scores, -1e30)
        attn_prob = jax.nn.softmax(scores, axis=-1).astype(jnp.bfloat16)
        blk_out = jnp.einsum('kgqs,skd->qkgd', attn_prob, v_blk, preferred_element_type=jnp.float32)
        return blk_out.astype(jnp.bfloat16)

    block_outs = lax.map(one_block, (jnp.arange(n_blocks), q_blocks, seg_blocks))
    return block_outs.reshape(n_query, loc_heads, head_dim)


def solution(mesh):
    num_tx = mesh.shape['tx']
    num_ty = mesh.shape['ty']
    width_spec = P('dp', ('tx', 'ty'))
    vec_spec = P(None, ('tx', 'ty'))
    proj_spec = P(None, 'tx', 'ty', None)
    head_spec = P(None, 'ty', None)
    cache_spec = P(None, ('dp', 'tx'), 'ty', None)
    in_specs = (width_spec, P('dp'), P('dp'), vec_spec, vec_spec, proj_spec, head_spec, proj_spec, head_spec,
                proj_spec, head_spec, P(None, 'ty', None, 'tx'), vec_spec, vec_spec, vec_spec,
                P(None, 'tx', 'ty'), P(None, ('ty', 'tx')), P(None, 'ty', 'tx'), vec_spec)
    out_specs = (width_spec, cache_spec, cache_spec)

    def device_fn(x_loc, seg_all, pos_all, ln1_gain, ln1_bias, w_q, b_q, w_k, b_k, w_v, b_v, w_o, b_o,
                  ln2_gain, ln2_bias, w_up, b_up, w_down, b_down):
        n_tok = x_loc.shape[0]
        tok_loc = n_tok // num_tx
        d_model = x_loc.shape[1] * num_tx * num_ty
        q_start = lax.axis_index('tx') * tok_loc
        seg_q = lax.dynamic_slice_in_dim(seg_all, q_start, tok_loc, 0)
        pos_q = lax.dynamic_slice_in_dim(pos_all, q_start, tok_loc, 0)
        cos_t, sin_t = rotary_tables(pos_q, w_q.shape[-1])
        hidden = x_loc
        k_list = []
        v_list = []
        for layer_idx in range(w_q.shape[0]):
            normed = norm_sharded(hidden, ln1_gain[layer_idx], ln1_bias[layer_idx], d_model)
            normed_rows = lax.all_gather(normed, 'ty', axis=1, tiled=True)
            q_part = jnp.einsum('td,dhe->the', normed_rows, w_q[layer_idx], preferred_element_type=jnp.float32)
            k_part = jnp.einsum('td,dhe->the', normed_rows, w_k[layer_idx], preferred_element_type=jnp.float32)
            v_part = jnp.einsum('td,dhe->the', normed_rows, w_v[layer_idx], preferred_element_type=jnp.float32)
            q_sum = lax.psum_scatter(q_part, 'tx', scatter_dimension=0, tiled=True)
            k_sum = lax.psum_scatter(k_part, 'tx', scatter_dimension=0, tiled=True)
            v_sum = lax.psum_scatter(v_part, 'tx', scatter_dimension=0, tiled=True)
            q_rot = rotary(q_sum + b_q[layer_idx].astype(jnp.float32), cos_t, sin_t).astype(jnp.bfloat16)
            k_new = rotary(k_sum + b_k[layer_idx].astype(jnp.float32), cos_t, sin_t).astype(jnp.bfloat16)
            v_new = (v_sum + b_v[layer_idx].astype(jnp.float32)).astype(jnp.bfloat16)
            k_all = lax.all_gather(k_new, 'tx', axis=0, tiled=True)
            v_all = lax.all_gather(v_new, 'tx', axis=0, tiled=True)
            attn_out = local_attention(q_rot, k_all, v_all, seg_q, seg_all, q_start)
            attn_rows = lax.all_gather(attn_out, 'tx', axis=0, tiled=True)
            o_part = jnp.einsum('the,hed->td', attn_rows, w_o[layer_idx], preferred_element_type=jnp.float32)
            o_sum = lax.psum_scatter(o_part, 'ty', scatter_dimension=1, tiled=True)
            hidden = (hidden.astype(jnp.float32) + o_sum + b_o[layer_idx].astype(jnp.float32)).astype(jnp.bfloat16)
            normed2 = norm_sharded(hidden, ln2_gain[layer_idx], ln2_bias[layer_idx], d_model)
            normed2_rows = lax.all_gather(normed2, 'ty', axis=1, tiled=True)
            up_part = jnp.dot(normed2_rows, w_up[layer_idx], preferred_element_type=jnp.float32)
            up_sum = lax.psum_scatter(up_part, 'tx', scatter_dimension=1, tiled=True)
            gelu_out = jax.nn.gelu(up_sum + b_up[layer_idx].astype(jnp.float32), approximate=True).astype(jnp.bfloat16)
            gelu_rows = lax.all_gather(gelu_out, 'tx', axis=1, tiled=True)
            down_part = jnp.dot(gelu_rows, w_down[layer_idx], preferred_element_type=jnp.float32)
            down_sum = lax.psum_scatter(down_part, 'ty', scatter_dimension=1, tiled=True)
            hidden = (hidden.astype(jnp.float32) + down_sum + b_down[layer_idx].astype(jnp.float32)).astype(jnp.bfloat16)
            k_list.append(k_new)
            v_list.append(v_new)
        return hidden, jnp.stack(k_list), jnp.stack(v_list)

    return jax.shard_map(device_fn, mesh=mesh, in_specs=in_specs, out_specs=out_specs, check_vma=False)
```

profile of v0, /device:TPU:97, one launch (start us, length us, event | category | flops | bytes accessed | tf_op | source)
XLA Modules:
  0.0 1623.4 jit_solution(17875439192011874318)
XLA Ops:
  8.5 50.0 %psum.28 = f32[2,4096]{1,0:T(2,128)S(1)} all-reduce(f32[2,4096]{1,0:T(2,128)S(1)} %pad_maximum_fusion.5), channel_id=1, replica_groups=mesh['dp'=1,'tx'=4,'ty'=8] {'tx','ty'}, use_global_device_ids=true, to_apply=%region_2.0 | all-reduce | flops 8192 | bytes 65536 | tf_op jit(solution)/shard_map/psum | solution.py:28
  139.9 45.1 %reduce-scatter.13.cloned.1.call-done = f32[1024,2,128]{2,0,1:T(8,128)} async-done(((f32[4096,2,128]{2,0,1:T(8,128)}), f32[1024,2,128]{2,0,1:T(8,128)}) %reduce-scatter.13.cloned.1.call-update) | async-done | bytes 1048592 | tf_op jit(solution)/shard_map/reduce_scatter | solution.py:96
  189.3 41.9 %reduce-scatter.17.cloned.1.call-done = f32[1024,2,128]{2,0,1:T(8,128)} async-done(((f32[4096,2,128]{2,0,1:T(8,128)}), f32[1024,2,128]{2,0,1:T(8,128)}) %reduce-scatter.17.cloned.1.call-update) | async-done | bytes 1048592 | tf_op jit(solution)/shard_map/reduce_scatter | solution.py:98
  260.9 30.0 %all-gather.17.cloned.1.call-done = bf16[4096,2,128]{2,0,1:T(8,128)(2,1)} async-done(((bf16[1024,2,128]{2,0,1:T(8,128)(2,1)}), bf16[4096,2,128]{2,0,1:T(8,128)(2,1)}) %all-gather.17.cloned.1.call-update) | async-done | bytes 2097168 | tf_op jit(solution)/shard_map/all_gather | solution.py:103
  291.1 53.4 %while.28 = (s32[]{:T(128)}, bf16[8,128,2,1,128]{4,1,0,2,3:T(8,128)(2,1)S(1)}, s32[8]{0:T(128)S(1)}, s32[]{:T(128)}, s32[8,128]{1,0:T(8,128)S(1)}, /*index=5*/s3...) while((s32[]{:T(128)}, ...), condition=%wide.region_9.10_spmd, body=%wide.region_6.9_spmd.sunk | while | flops 548441728 | bytes 26403056 | solution.py:61
  345.4 28.1 %all-gather.19.cloned.1.call-done = bf16[4096,2,128]{2,0,1:T(8,128)(2,1)} async-done(((bf16[1024,2,128]{2,0,1:T(8,128)(2,1)}), bf16[4096,2,128]{2,0,1:T(8,128)(2,1)}) %all-gather.19.cloned.1.call-update) | async-done | bytes 2097168 | tf_op jit(solution)/shard_map/all_gather | solution.py:105
  380.4 49.2 %reduce-scatter.19.cloned.1.call-done = f32[4096,64]{0,1:T(8,128)} async-done(((f32[4096,512]{0,1:T(8,128)}), f32[4096,64]{0,1:T(8,128)}) %reduce-scatter.19.cloned.1.call-update) | async-done | bytes 1048592 | tf_op jit(solution)/shard_map/reduce_scatter | solution.py:107
  431.2 45.8 %psum.29 = f32[2,4096]{1,0:T(2,128)S(1)} all-reduce(f32[2,4096]{1,0:T(2,128)S(1)} %pad_maximum_fusion.6), channel_id=1, replica_groups=mesh['dp'=1,'tx'=4,'ty'=8] {'tx','ty'}, use_global_device_ids=true, to_apply=%region_13.14 | all-reduce | flops 8192 | bytes 65536 | tf_op jit(solution)/shard_map/psum | solution.py:28
  478.1 27.4 %all-gather.21.cloned.1.call-done = bf16[4096,512]{0,1:T(8,128)(2,1)} async-done(((bf16[4096,64]{0,1:T(8,128)(2,1)}), bf16[4096,512]{0,1:T(8,128)(2,1)}) %all-gather.21.cloned.1.call-update) | async-done | bytes 4194320 | tf_op jit(solution)/shard_map/all_gather | solution.py:110
  519.1 144.3 %reduce-scatter.21.cloned.1.call-done = f32[4096,256]{1,0:T(8,128)} async-done(((f32[4096,1024]{1,0:T(8,128)}), f32[4096,256]{1,0:T(8,128)}) %reduce-scatter.21.cloned.1.call-update) | async-done | bytes 4194320 | tf_op jit(solution)/shard_map/reduce_scatter | solution.py:112
  668.4 82.8 %all-gather.23.cloned.1.call-done = bf16[4096,1024]{1,0:T(8,128)(2,1)} async-done(((bf16[4096,256]{1,0:T(8,128)(2,1)}), bf16[4096,1024]{1,0:T(8,128)(2,1)}) %all-gather.23.cloned.1.call-update) | async-done | bytes 8388624 | tf_op jit(solution)/shard_map/all_gather | solution.py:114
  763.4 50.7 %reduce-scatter.23.cloned.1.call-done = f32[4096,64]{0,1:T(8,128)} async-done(((f32[4096,512]{0,1:T(8,128)}), f32[4096,64]{0,1:T(8,128)}) %reduce-scatter.23.cloned.1.call-update) | async-done | bytes 1048592 | tf_op jit(solution)/shard_map/reduce_scatter | solution.py:116
  815.7 45.7 %psum.30 = f32[2,4096]{1,0:T(2,128)S(1)} all-reduce(f32[2,4096]{1,0:T(2,128)S(1)} %pad_maximum_fusion.7), channel_id=1, replica_groups=mesh['dp'=1,'tx'=4,'ty'=8] {'tx','ty'}, use_global_device_ids=true, to_apply=%region_18.19 | all-reduce | flops 8192 | bytes 65536 | tf_op jit(solution)/shard_map/psum | solution.py:28
  907.7 31.7 %reduce-scatter.25.cloned.1.call-done = f32[1024,2,128]{2,0,1:T(8,128)} async-done(((f32[4096,2,128]{2,0,1:T(8,128)}), f32[1024,2,128]{2,0,1:T(8,128)}) %reduce-scatter.25.cloned.1.call-update) | async-done | bytes 1048592 | tf_op jit(solution)/shard_map/reduce_scatter | solution.py:96
  940.7 44.9 %reduce-scatter.27.cloned.1.call-done = f32[1024,2,128]{2,0,1:T(8,128)} async-done(((f32[4096,2,128]{2,0,1:T(8,128)}), f32[1024,2,128]{2,0,1:T(8,128)}) %reduce-scatter.27.cloned.1.call-update) | async-done | bytes 1048592 | tf_op jit(solution)/shard_map/reduce_scatter | solution.py:97
  989.9 42.0 %reduce-scatter.29.cloned.1.call-done = f32[1024,2,128]{2,0,1:T(8,128)} async-done(((f32[4096,2,128]{2,0,1:T(8,128)}), f32[1024,2,128]{2,0,1:T(8,128)}) %reduce-scatter.29.cloned.1.call-update) | async-done | bytes 1048592 | tf_op jit(solution)/shard_map/reduce_scatter | solution.py:98
  1061.6 29.5 %all-gather.29.cloned.1.call-done = bf16[4096,2,128]{2,0,1:T(8,128)(2,1)} async-done(((bf16[1024,2,128]{2,0,1:T(8,128)(2,1)}), bf16[4096,2,128]{2,0,1:T(8,128)(2,1)}) %all-gather.29.cloned.1.call-update) | async-done | bytes 2097168 | tf_op jit(solution)/shard_map/all_gather | solution.py:103
  1091.2 53.2 %while.29 = (s32[]{:T(128)}, bf16[8,128,2,1,128]{4,1,0,2,3:T(8,128)(2,1)S(1)}, s32[8]{0:T(128)S(1)}, s32[]{:T(128)}, s32[8,128]{1,0:T(8,128)S(1)}, /*index=5*/s3...) while((s32[]{:T(128)}, ...), condition=%wide.region_25.26_spmd, body=%wide.region_22.25_spmd.sunk | while | flops 548441728 | bytes 26402548 | solution.py:61
  1145.3 28.1 %all-gather.31.cloned.1.call-done = bf16[4096,2,128]{2,0,1:T(8,128)(2,1)} async-done(((bf16[1024,2,128]{2,0,1:T(8,128)(2,1)}), bf16[4096,2,128]{2,0,1:T(8,128)(2,1)}) %all-gather.31.cloned.1.call-update) | async-done | bytes 2097168 | tf_op jit(solution)/shard_map/all_gather | solution.py:105
  1179.6 49.8 %reduce-scatter.31.cloned.1.call-done = f32[4096,64]{0,1:T(8,128)} async-done(((f32[4096,512]{0,1:T(8,128)}), f32[4096,64]{0,1:T(8,128)}) %reduce-scatter.31.cloned.1.call-update) | async-done | bytes 1048592 | tf_op jit(solution)/shard_map/reduce_scatter | solution.py:107
  1231.0 45.8 %psum.31 = f32[2,4096]{1,0:T(2,128)S(1)} all-reduce(f32[2,4096]{1,0:T(2,128)S(1)} %pad_maximum_fusion.8), channel_id=1, replica_groups=mesh['dp'=1,'tx'=4,'ty'=8] {'tx','ty'}, use_global_device_ids=true, to_apply=%region_29.30 | all-reduce | flops 8192 | bytes 65536 | tf_op jit(solution)/shard_map/psum | solution.py:28
  1318.4 144.8 %reduce-scatter.33.cloned.1.call-done = f32[4096,256]{1,0:T(8,128)} async-done(((f32[4096,1024]{1,0:T(8,128)}), f32[4096,256]{1,0:T(8,128)}) %reduce-scatter.33.cloned.1.call-update) | async-done | bytes 4194320 | tf_op jit(solution)/shard_map/reduce_scatter | solution.py:112
  1468.6 82.5 %all-gather.35.cloned.1.call-done = bf16[4096,1024]{1,0:T(8,128)(2,1)} async-done(((bf16[4096,256]{1,0:T(8,128)(2,1)}), bf16[4096,1024]{1,0:T(8,128)(2,1)}) %all-gather.35.cloned.1.call-update) | async-done | bytes 8388624 | tf_op jit(solution)/shard_map/all_gather | solution.py:114
  1569.5 44.4 %reduce-scatter.35.cloned.1.call-done = f32[4096,64]{0,1:T(8,128)} async-done(((f32[4096,512]{0,1:T(8,128)}), f32[4096,64]{0,1:T(8,128)}) %reduce-scatter.35.cloned.1.call-update) | async-done | bytes 1048592 | tf_op jit(solution)/shard_map/reduce_scatter | solution.py:116
  (344 shorter events, 412.0 us)
Async XLA Ops:
  7.2 82.0 %all-gather.13.cloned.1.call-start = ((), (), s32[]{:S(2)}) async-start(), calls=%async_computation.12 | async-start | bytes 4718592 | tf_op jit(solution)/shard_map/all_gather | solution.py:92
  61.4 77.2 %reduce-scatter.15.cloned.1.call-start = ((), (), s32[]{:S(2)}) async-start(), calls=%async_computation.14 | async-start | bytes 5242880 | tf_op jit(solution)/shard_map/reduce_scatter | solution.py:97
  94.8 90.2 %reduce-scatter.13.cloned.1.call-start = ((), (), s32[]{:S(2)}) async-start(), calls=%async_computation.13 | async-start | bytes 5242880 | tf_op jit(solution)/shard_map/reduce_scatter | solution.py:96
  102.4 128.8 %reduce-scatter.17.cloned.1.call-start = ((), (), s32[]{:S(2)}) async-start(), calls=%async_computation.16 | async-start | bytes 5242880 | tf_op jit(solution)/shard_map/reduce_scatter | solution.py:98
  110.0 150.9 %all-gather.15.cloned.1.call-start = ((), (), s32[]{:S(2)}) async-start(), calls=%async_computation.15 | async-start | bytes 2621440 | tf_op jit(solution)/shard_map/all_gather | solution.py:102
  189.1 101.8 %all-gather.17.cloned.1.call-start = ((), (), s32[]{:S(2)}) async-start(), calls=%async_computation.17 | async-start | bytes 2621440 | tf_op jit(solution)/shard_map/all_gather | solution.py:103
  233.3 140.2 %all-gather.19.cloned.1.call-start = ((), (), s32[]{:S(2)}) async-start(), calls=%async_computation.18 | async-start | bytes 2621440 | tf_op jit(solution)/shard_map/all_gather | solution.py:105
  345.3 84.2 %reduce-scatter.19.cloned.1.call-start = ((), (), s32[]{:S(2)}) async-start(), calls=%async_computation.19 | async-start | bytes 9437184 | tf_op jit(solution)/shard_map/reduce_scatter | solution.py:107
  379.7 125.8 %all-gather.21.cloned.1.call-start = ((), (), s32[]{:S(2)}) async-start(), calls=%async_computation.20 | async-start | bytes 4718592 | tf_op jit(solution)/shard_map/all_gather | solution.py:110
  478.1 185.3 %reduce-scatter.21.cloned.1.call-start = ((), (), s32[]{:S(2)}) async-start(), calls=%async_computation.21 | async-start | bytes 20971520 | tf_op jit(solution)/shard_map/reduce_scatter | solution.py:112
  518.5 232.8 %all-gather.23.cloned.1.call-start = ((), (), s32[]{:S(2)}) async-start(), calls=%async_computation.22 | async-start | bytes 10485760 | tf_op jit(solution)/shard_map/all_gather | solution.py:114
  668.4 145.7 %reduce-scatter.23.cloned.1.call-start = ((), (), s32[]{:S(2)}) async-start(), calls=%async_computation.23 | async-start | bytes 9437184 | tf_op jit(solution)/shard_map/reduce_scatter | solution.py:116
  762.8 127.3 %all-gather.25.cloned.1.call-start = ((), (), s32[]{:S(2)}) async-start(), calls=%async_computation.24 | async-start | bytes 4718592 | tf_op jit(solution)/shard_map/all_gather | solution.py:92
  862.5 76.9 %reduce-scatter.25.cloned.1.call-start = ((), (), s32[]{:S(2)}) async-start(), calls=%async_computation.25 | async-start | bytes 5242880 | tf_op jit(solution)/shard_map/reduce_scatter | solution.py:96
  895.6 90.0 %reduce-scatter.27.cloned.1.call-start = ((), (), s32[]{:S(2)}) async-start(), calls=%async_computation.26 | async-start | bytes 5242880 | tf_op jit(solution)/shard_map/reduce_scatter | solution.py:97
  901.3 130.6 %reduce-scatter.29.cloned.1.call-start = ((), (), s32[]{:S(2)}) async-start(), calls=%async_computation.28 | async-start | bytes 5242880 | tf_op jit(solution)/shard_map/reduce_scatter | solution.py:98
  907.6 154.0 %all-gather.27.cloned.1.call-start = ((), (), s32[]{:S(2)}) async-start(), calls=%async_computation.27 | async-start | bytes 2621440 | tf_op jit(solution)/shard_map/all_gather | solution.py:102
  989.8 101.3 %all-gather.29.cloned.1.call-start = ((), (), s32[]{:S(2)}) async-start(), calls=%async_computation.29 | async-start | bytes 2621440 | tf_op jit(solution)/shard_map/all_gather | solution.py:103
  1034.1 139.3 %all-gather.31.cloned.1.call-start = ((), (), s32[]{:S(2)}) async-start(), calls=%async_computation.30 | async-start | bytes 2621440 | tf_op jit(solution)/shard_map/all_gather | solution.py:105
  1145.2 84.2 %reduce-scatter.31.cloned.1.call-start = ((), (), s32[]{:S(2)}) async-start(), calls=%async_computation.31 | async-start | bytes 9437184 | tf_op jit(solution)/shard_map/reduce_scatter | solution.py:107
  1179.6 125.8 %all-gather.33.cloned.1.call-start = ((), (), s32[]{:S(2)}) async-start(), calls=%async_computation.32 | async-start | bytes 4718592 | tf_op jit(solution)/shard_map/all_gather | solution.py:110
  1277.9 185.3 %reduce-scatter.33.cloned.1.call-start = ((), (), s32[]{:S(2)}) async-start(), calls=%async_computation.33 | async-start | bytes 20971520 | tf_op jit(solution)/shard_map/reduce_scatter | solution.py:112
  1318.3 232.8 %all-gather.35.cloned.1.call-start = ((), (), s32[]{:S(2)}) async-start(), calls=%async_computation.34 | async-start | bytes 10485760 | tf_op jit(solution)/shard_map/all_gather | solution.py:114
  1468.2 145.7 %reduce-scatter.35.cloned.1.call-start = ((), (), s32[]{:S(2)}) async-start(), calls=%async_computation.35 | async-start | bytes 9437184 | tf_op jit(solution)/shard_map/reduce_scatter | solution.py:116
  (45 other events, 792.5 us)
Sparse Core Ops, SparseCore 0:
  61.5 27.6 all-gather.12
  94.9 43.6 reduce-scatter.14
  140.9 44.0 reduce-scatter.12
  187.1 44.0 reduce-scatter.16
  233.2 27.6 all-gather.14
  262.9 27.9 all-gather.16
  345.5 27.9 all-gather.18
  379.9 49.6 reduce-scatter.18
  478.2 27.3 all-gather.20
  518.6 144.7 reduce-scatter.20
  668.5 82.7 all-gather.22
  762.9 51.1 reduce-scatter.22
  862.7 27.3 all-gather.24
  895.7 43.6 reduce-scatter.24
  941.6 44.0 reduce-scatter.26
  987.8 44.0 reduce-scatter.28
  1033.9 27.6 all-gather.26
  1063.0 27.9 all-gather.28
  1145.3 27.9 all-gather.30
  1179.7 49.6 reduce-scatter.30
  1278.0 27.3 all-gather.32
  1318.4 144.7 reduce-scatter.32
  1468.3 82.6 all-gather.34
  1562.8 51.1 reduce-scatter.34
where the time goes:
time: 1630 us; the launch traced here: 1620 us
  waiting for transfers between devices  1160 us (71%)
  blocking collectives  187 us (11%)
  matrix products  157 us (10%)
  other arithmetic  66.8 us (4%)
  local copies, waits for them, and re-layouts  24.3 us (1%)
    reduce_scatter x2, waiting for transfers between devices, device_fn(): up_sum = lax.psum_scatter(up_part, 'tx', scatter_dimension=1, tiled=True)  289 us
    psum x4, blocking collectives, norm_sharded(): norm_sums = lax.psum(local_sums, ('tx', 'ty'))  187 us
    all_gather x2, waiting for transfers between devices, device_fn(): gelu_rows = lax.all_gather(gelu_out, 'tx', axis=1, tiled=True)  165 us
    reduce_scatter x2, waiting for transfers between devices, device_fn(): o_sum = lax.psum_scatter(o_part, 'ty', scatter_dimension=1, tiled=True)  99 us
    reduce_scatter x2, waiting for transfers between devices, device_fn(): lax.psum_scatter(down_part, 'ty', scatter_dimension=1, tiled=True)  95.1 us
    reduce_scatter x2, waiting for transfers between devices, device_fn(): v_sum = lax.psum_scatter(v_part, 'tx', scatter_dimension=0, tiled=True)  83.9 us
    reduce_scatter x2, waiting for transfers between devices, device_fn(): q_sum = lax.psum_scatter(q_part, 'tx', scatter_dimension=0, tiled=True)  76.8 us
    reduce_scatter x2, waiting for transfers between devices, device_fn(): k_sum = lax.psum_scatter(k_part, 'tx', scatter_dimension=0, tiled=True)  70.8 us
  transfers between devices with their start and end apart: 24, of which 24 were waited for; matrix products, arithmetic and copies ran while one was open for 3% of the time, Pallas kernels for 0%

commit v1 on v0

v1 whole, which is shorter than its diff:
```python
import math
import functools
import jax
import jax.numpy as jnp
from jax import lax
from jax.experimental import pallas as pl
from jax.experimental.pallas import tpu as pltpu
from jax.sharding import PartitionSpec as P

MESH = pl.DeviceIdType.MESH
F32 = jnp.float32
BF16 = jnp.bfloat16
ROPE_THETA = 100000.0
BK = 256
LOG2E = 1.4426950408889634


def rows_norm(x_f32, gain, bias):
    width = x_f32.shape[-1]
    mean = jnp.sum(x_f32, axis=-1, keepdims=True) / width
    var = jnp.sum(x_f32 * x_f32, axis=-1, keepdims=True) / width - mean * mean
    normed = (x_f32 - mean) * lax.rsqrt(var + 1e-5)
    return (normed * gain.astype(F32) + bias.astype(F32)).astype(BF16)


class Ring:
    def __init__(self, num_tx, num_ty):
        self.ty = lax.axis_index('ty')
        self.y = lax.axis_index('tx')
        self.num_tx, self.num_ty = num_tx, num_ty
        self.n_chip = num_ty // 2
        self.x = self.ty // 2
        self.c = self.ty % 2

    def side(self, k):
        return lax.rem(self.y + k, self.num_tx)

    def chip(self, k):
        return lax.rem(self.x + k, self.n_chip)

    def peer(self, k):
        return {'ty': self.chip(k) * 2 + self.c}

    def sibling(self):
        return {'ty': self.x * 2 + (1 - self.c)}


def remote(src, dst, send_sem, recv_sem, to):
    return pltpu.make_async_remote_copy(src_ref=src, dst_ref=dst, send_sem=send_sem, recv_sem=recv_sem, device_id=to,
                                        device_id_type=MESH)


def at(y, ty):
    return {'tx': y, 'ty': ty}


def signal(to):
    pl.semaphore_signal(pltpu.get_barrier_semaphore(), inc=1, device_id=to, device_id_type=MESH)


def copy_or_send(here, src, dst, send_sem, recv_sem, to):
    @pl.when(here)
    def _():
        pltpu.make_async_copy(src, dst, recv_sem).start()

    @pl.when(jnp.logical_not(here))
    def _():
        remote(src, dst, send_sem, recv_sem, to).start()


def sent(here, src, dst, send_sem, recv_sem, to):
    @pl.when(jnp.logical_not(here))
    def _():
        remote(src, dst, send_sem, recv_sem, to).wait_send()


AG_SIB, AG_R0, AG_R1, AG_L1, AG_L0, AG_FR, AG_FL = 0, 1, 2, 3, 4, 5, 6
AG_SL, AG_SR, AG_SO0, AG_SO1 = 7, 8, 9, 10
AG_SEMS = 11


class RowGather:
    def __init__(self, ring, buf, sems, rows):
        r = ring
        half = rows // 2
        mine, other = r.c * rows, (1 - r.c) * rows
        right, left, far = r.chip(1), r.chip(r.n_chip - 1), r.chip(2)

        def cp(slot, i, off, n, to):
            ref = buf.at[slot, pl.ds(pl.multiple_of(off, 16), n)]
            return remote(ref, ref, sems.at[0, i], sems.at[1, i], to)

        sib, to_r, to_l = r.sibling(), r.peer(1), r.peer(r.n_chip - 1)
        self.s_sib = cp(r.x, AG_SIB, mine, rows, sib)
        self.s_r0 = cp(r.x, AG_R0, mine, half, to_r)
        self.s_r1 = cp(r.x, AG_R1, mine + half, half, to_r)
        self.s_l1 = cp(r.x, AG_L1, mine + half, half, to_l)
        self.s_l0 = cp(r.x, AG_L0, mine, half, to_l)
        self.s_fr = cp(left, AG_FR, mine, half, to_r)
        self.s_fl = cp(right, AG_FL, mine + half, half, to_l)
        self.s_sl = cp(left, AG_SL, mine, rows, sib)
        self.s_sr = cp(right, AG_SR, mine, rows, sib)
        self.s_so0 = cp(far, AG_SO0, mine, half, sib)
        self.s_so1 = cp(far, AG_SO1, mine + half, half, sib)
        self.r_sib = cp(r.x, AG_SIB, other, rows, sib)
        self.r_r0 = cp(left, AG_R0, mine, half, to_r)
        self.r_r1 = cp(left, AG_R1, mine + half, half, to_r)
        self.r_l1 = cp(right, AG_L1, mine + half, half, to_l)
        self.r_l0 = cp(right, AG_L0, mine, half, to_l)
        self.r_fr = cp(far, AG_FR, mine, half, to_r)
        self.r_fl = cp(far, AG_FL, mine + half, half, to_l)
        self.r_sl = cp(left, AG_SL, other, rows, sib)
        self.r_sr = cp(right, AG_SR, other, rows, sib)
        self.r_so0 = cp(far, AG_SO0, other, half, sib)
        self.r_so1 = cp(far, AG_SO1, other + half, half, sib)

    def start(self):
        for s in (self.s_sib, self.s_r0, self.s_l1, self.s_r1, self.s_l0):
            s.start()

    def own(self):
        self.r_sib.wait_recv()

    def relay(self):
        self.r_r0.wait_recv()
        self.s_fr.start()
        self.r_l1.wait_recv()
        self.s_fl.start()

    def near(self):
        self.r_r1.wait_recv()
        self.s_sl.start()
        self.r_l0.wait_recv()
        self.s_sr.start()

    def near_left(self):
        self.r_sl.wait_recv()

    def near_right(self):
        self.r_sr.wait_recv()

    def far(self):
        self.r_fr.wait_recv()
        self.s_so0.start()
        self.r_fl.wait_recv()
        self.s_so1.start()
        self.r_so0.wait_recv()
        self.r_so1.wait_recv()

    def finish(self):
        for s in (self.s_sib, self.s_r0, self.s_r1, self.s_l1, self.s_l0, self.s_fr, self.s_fl, self.s_sl, self.s_sr,
                  self.s_so0, self.s_so1):
            s.wait_send()


def gelu_tanh(x):
    return 0.5 * x * (1.0 + jnp.tanh(0.7978845608028654 * (x + 0.044715 * (x * x * x))))


RS_SIB, RS_B, RS_A, RS_OA, RS_OB, RS_SA, RS_SB = 0, 4, 5, 6, 7, 8, 9
RS_SEMS = 10


def mlp_kernel(num_tx, num_ty, o_hbm, hid_ref, wo_hbm, wu_hbm, wd_hbm, bo_ref, g2_ref, b2_ref, bu_ref, bd_ref, y_ref,
               wo, wu, wd, obuf, u_all, x1, g_ref, full, sibin, far_in, fin, w_sems, a_sems, g_sems, r_sems):
    ring = Ring(num_tx, num_ty)
    rows, width = hid_ref.shape
    head_w = o_hbm.shape[1]
    n_col = wo_hbm.shape[0]
    col_w = wo_hbm.shape[2]
    half_w = width // 2
    n_chip = ring.n_chip
    last = n_chip - 1
    x, y, c = ring.x, ring.y, ring.c
    loads = [pltpu.make_async_copy(wo_hbm, wo, w_sems.at[0]), pltpu.make_async_copy(wu_hbm, wu, w_sems.at[1]),
             pltpu.make_async_copy(wd_hbm, wd, w_sems.at[2])]
    for ld in loads:
        ld.start()

    par = lax.rem(x, 2)
    targets, sources = [], []
    for dy in range(num_tx):
        for dx in range(n_chip // 2):
            for dc in range(2):
                targets.append((ring.side(dy), lax.rem(x // 2 + dx, n_chip // 2) * 2 + c, lax.rem(c + dc, 2)))
        for dx in range(n_chip):
            sources.append((ring.side(num_tx - dy), lax.rem(x + n_chip - dx, n_chip)))
    for ys, xs in sources[1:]:
        signal(at(ys, xs * 2 + par))

    @pl.when(par != c)
    def _():
        signal(ring.sibling())
    for to in (ring.sibling(), ring.peer(1), ring.peer(last)):
        signal(to)
    n_far = len(targets) - 1
    barrier = pltpu.get_barrier_semaphore()

    @pl.when(par == c)
    def _():
        pl.semaphore_wait(barrier, n_far + 3)

    @pl.when(par != c)
    def _():
        pl.semaphore_wait(barrier, n_far + 4)

    head_cols = pl.ds(pl.multiple_of((x * num_tx + y) * head_w, head_w), head_w)
    here = par == c

    def o_piece(n):
        yt, xt, ct = targets[n]
        at_row = (yt * (n_chip // 2) + xt // 2) * (2 * rows) + ct * rows
        return (o_hbm.at[pl.ds(pl.multiple_of(at_row, rows), rows)], obuf.at[:, head_cols], a_sems.at[0, n],
                a_sems.at[1, y * n_chip + x], at(yt, xt * 2 + ct))
    for n in list(range(1, len(targets))) + [0]:
        if n == 0:
            copy_or_send(here, *o_piece(n))
        else:
            remote(*o_piece(n)).start()
    loads[0].wait()
    for ys in range(num_tx):
        for xs in range(n_chip):
            remote(o_hbm.at[pl.ds(0, rows)], obuf.at[:, pl.ds((xs * num_tx + ys) * head_w, head_w)], a_sems.at[0, 0],
                   a_sems.at[1, ys * n_chip + xs], ring.sibling()).wait_recv()

    def project(t, carry):
        cols = pl.ds(pl.multiple_of(t * col_w, col_w), col_w)
        x1[:, cols] = (hid_ref[:, cols].astype(F32) + jnp.dot(obuf[...], wo[t], preferred_element_type=F32)
                       + bo_ref[:, cols].astype(F32)).astype(BF16)
        return carry
    lax.fori_loop(0, n_col, project, 0)
    u_all[ring.x, pl.ds(pl.multiple_of(c * rows, rows), rows), :] = rows_norm(x1[...].astype(F32), g2_ref[...], b2_ref[...])

    gather = RowGather(ring, u_all, g_sems, rows)
    gather.start()
    loads[1].wait()
    loads[2].wait()

    mine = pl.ds(pl.multiple_of(c * rows, rows), rows)
    other = pl.ds(pl.multiple_of((1 - c) * rows, rows), rows)
    sib = [remote(full.at[k, other], sibin.at[k], r_sems.at[0, RS_SIB + k], r_sems.at[1, RS_SIB + k], ring.sibling()) for k in range(4)]

    def mlp(k):
        slot = ring.chip(k)
        n_up = wu.shape[1] // 512

        def up(n, carry):
            cols = pl.ds(pl.multiple_of(n * 512, 512), 512)
            h = jnp.dot(u_all[slot], wu[:, cols], preferred_element_type=F32) + bu_ref[:, cols].astype(F32)
            g_ref[:, cols] = gelu_tanh(h).astype(BF16)
            return carry
        lax.fori_loop(0, n_up, up, 0)

        def down(t, carry):
            full[k, :, pl.ds(pl.multiple_of(t * col_w, col_w), col_w)] = jnp.dot(g_ref[...], wd[t], preferred_element_type=F32)
            return carry
        lax.fori_loop(0, n_col, down, 0)
        sib[k].start()

    def add_half(k, lo, src):
        cols = pl.ds(lo, half_w)
        full[k, mine, cols] = full[k, mine, cols] + src

    left_h, right_h = pl.ds(0, half_w), pl.ds(half_w, half_w)
    to_r, to_l = ring.peer(1), ring.peer(last)
    s_b = remote(full.at[1, mine, right_h], fin.at[0], r_sems.at[0, RS_B], r_sems.at[1, RS_B], to_r)
    s_a = remote(full.at[3, mine, left_h], fin.at[1], r_sems.at[0, RS_A], r_sems.at[1, RS_A], to_l)
    s_oa = remote(full.at[2, mine, left_h], far_in.at[0], r_sems.at[0, RS_OA], r_sems.at[1, RS_OA], to_r)
    s_ob = remote(full.at[2, mine, right_h], far_in.at[1], r_sems.at[0, RS_OB], r_sems.at[1, RS_OB], to_l)
    s_sa = remote(full.at[1, mine, left_h], fin.at[2], r_sems.at[0, RS_SA], r_sems.at[1, RS_SA], to_r)
    s_sb = remote(full.at[3, mine, right_h], fin.at[3], r_sems.at[0, RS_SB], r_sems.at[1, RS_SB], to_l)

    def pair_sum(k):
        sib[k].wait_recv()
        full[k, mine] = full[k, mine] + sibin[k]

    gather.own()
    mlp(0)
    gather.relay()
    gather.near()
    gather.near_right()
    mlp(1)
    gather.near_left()
    pair_sum(1)
    s_b.start()
    mlp(3)
    gather.far()
    pair_sum(3)
    s_a.start()
    mlp(2)
    pair_sum(0)
    pair_sum(2)
    s_oa.start()
    s_ob.start()
    x1_f = x1[...].astype(F32) + bd_ref[...].astype(F32)
    full[0, mine] = full[0, mine] + x1_f
    s_oa.wait_recv()
    add_half(1, 0, far_in[0])
    s_sa.start()
    s_ob.wait_recv()
    add_half(3, half_w, far_in[1])
    s_sb.start()
    s_b.wait_recv()
    add_half(0, half_w, fin[0])
    s_a.wait_recv()
    add_half(0, 0, fin[1])
    s_sa.wait_recv()
    y_ref[:, left_h] = (full[0, mine, left_h] + fin[2]).astype(BF16)
    s_sb.wait_recv()
    y_ref[:, right_h] = (full[0, mine, right_h] + fin[3]).astype(BF16)
    for n in range(1, len(targets)):
        remote(*o_piece(n)).wait_send()
    sent(here, *o_piece(0))
    for s in sib + [s_b, s_a, s_oa, s_ob, s_sa, s_sb]:
        s.wait_send()
    gather.finish()


def mlp_call(num_tx, num_ty, o, hid, wo, wu, wd, bo, g2, b2, bu, bd, cid):
    rows, width = hid.shape
    n_chip = num_ty // 2
    vm = pl.BlockSpec(memory_space=pltpu.VMEM)
    hb = pl.BlockSpec(memory_space=pl.ANY)
    half_w = width // 2
    ff = wu.shape[1]
    dma = pltpu.SemaphoreType.DMA
    return pl.pallas_call(
        functools.partial(mlp_kernel, num_tx, num_ty),
        out_shape=jax.ShapeDtypeStruct((rows, width), BF16),
        in_specs=[hb, vm, hb, hb, hb] + [vm] * 5,
        out_specs=vm,
        scratch_shapes=[pltpu.VMEM(wo.shape, BF16), pltpu.VMEM(wu.shape, BF16), pltpu.VMEM(wd.shape, BF16),
                        pltpu.VMEM((rows, width), BF16), pltpu.VMEM((n_chip, 2 * rows, width), BF16),
                        pltpu.VMEM((rows, width), BF16), pltpu.VMEM((2 * rows, ff), BF16),
                        pltpu.VMEM((n_chip, 2 * rows, width), F32), pltpu.VMEM((n_chip, rows, width), F32),
                        pltpu.VMEM((2, rows, half_w), F32), pltpu.VMEM((4, rows, half_w), F32),
                        dma((4,)), dma((2, num_tx * n_chip)), dma((2, AG_SEMS)), dma((2, RS_SEMS))],
        compiler_params=pltpu.CompilerParams(collective_id=cid, has_side_effects=True, vmem_limit_bytes=56 << 20),
        cost_estimate=pl.CostEstimate(flops=80_000_000_000, bytes_accessed=20 << 20, transcendentals=0),
        name="mlp",
    )(o, hid, wo, wu, wd, bo, g2, b2, bu, bd)


def qkv_kernel(num_tx, num_ty, hid_ref, g1_ref, b1_ref, wq_hbm, wk_hbm, wv_hbm, bq_ref, bk_ref, bv_ref, cos_ref, sin_ref,
               kc_ref, vc_ref, kv_hbm, qh_hbm, w, a_all, st, w_sems, g_sems, snd_sems, kv_sems, q_sems, f_sems):
    ring = Ring(num_tx, num_ty)
    rows, width = hid_ref.shape
    loc_w = wq_hbm.shape[1]
    head_w = kv_hbm.shape[2]
    loc_heads = loc_w // head_w
    n_chip = ring.n_chip
    last = n_chip - 1
    blk = 2 * rows
    x, y, c = ring.x, ring.y, ring.c
    loads = [pltpu.make_async_copy(src, w.at[:, pl.ds(i * loc_w, loc_w)], w_sems.at[i])
             for i, src in enumerate((wq_hbm, wk_hbm, wv_hbm))]
    for ld in loads:
        ld.start()

    src_core = y // loc_heads
    for dy in range(1, num_tx):
        signal(at(ring.side(dy), x * 2 + src_core))

    @pl.when(src_core != c)
    def _():
        signal(ring.sibling())
    for to in (ring.sibling(), ring.peer(1), ring.peer(last)):
        signal(to)
    barrier = pltpu.get_barrier_semaphore()

    @pl.when(src_core == c)
    def _():
        pl.semaphore_wait(barrier, 2 * loc_heads - 1 + 3)

    @pl.when(src_core != c)
    def _():
        pl.semaphore_wait(barrier, 2 * loc_heads + 3)

    a_all[x, pl.ds(pl.multiple_of(c * rows, rows), rows), :] = rows_norm(hid_ref[...].astype(F32), g1_ref[...], b1_ref[...])
    gather = RowGather(ring, a_all, g_sems, rows)
    gather.start()
    for ld in loads:
        ld.wait()

    def block_rows(ys, slot):
        return pl.ds(pl.multiple_of((ys * n_chip + slot) * blk, blk), blk)

    def pieces(k):
        slot = ring.chip(k)
        out = []
        for h in range(loc_heads):
            yd = c * loc_heads + h
            for r in range(2):
                here = jnp.logical_and(yd == y, c == r)
                out.append((here, st.at[k, h, r], kv_hbm.at[r, block_rows(y, slot)], snd_sems.at[(k * loc_heads + h) * 3 + r],
                            kv_sems.at[y * n_chip + slot], at(yd, x * 2 + r)))
            par = lax.rem(slot, 2)
            q_at = y * (n_chip // 2) + slot // 2
            here = jnp.logical_and(yd == y, c == par)
            out.append((here, st.at[k, h, 2], qh_hbm.at[pl.ds(pl.multiple_of(q_at * blk, blk), blk)],
                        snd_sems.at[(k * loc_heads + h) * 3 + 2], q_sems.at[q_at], at(yd, x * 2 + par)))
        return out

    def project(k):
        slot = ring.chip(k)
        at_row = pl.ds(pl.multiple_of(slot * blk, blk), blk)
        acc = jnp.dot(a_all[slot], w[...], preferred_element_type=F32)
        cos_t, sin_t = cos_ref[at_row, :], sin_ref[at_row, :]

        def turned(i, h, bias_ref):
            lanes = slice(h * head_w, (h + 1) * head_w)
            v = acc[:, i * loc_w + h * head_w:i * loc_w + (h + 1) * head_w] + bias_ref[:, lanes].astype(F32)
            if i < 2:
                v = v * cos_t + pltpu.roll(v, head_w // 2, 1) * sin_t
            return v.astype(BF16)
        for h in range(loc_heads):
            lanes = slice(h * head_w, (h + 1) * head_w)
            st[k, h, 2] = turned(0, h, bq_ref)
            k_new = turned(1, h, bk_ref)
            st[k, h, 0] = k_new
            kc_ref[at_row, lanes] = k_new
            v_new = turned(2, h, bv_ref)
            st[k, h, 1] = v_new
            vc_ref[at_row, lanes] = v_new
        for p in pieces(k):
            copy_or_send(*p)

    gather.own()
    project(0)
    gather.relay()
    gather.near()
    gather.near_right()
    project(1)
    gather.near_left()
    project(last)
    gather.far()
    project(2)

    def forward(i, r):
        ref = kv_hbm.at[r, pl.ds(pl.multiple_of(i * blk, blk), blk)]
        return remote(ref, ref, f_sems.at[0, i], f_sems.at[1, i], ring.sibling())

    for k in (0, 1, last, 2):
        for dy in (0, 1, num_tx - 1, 2):
            i = ring.side(dy) * n_chip + ring.chip(k)
            remote(st.at[0, 0, 0], kv_hbm.at[c, pl.ds(pl.multiple_of(i * blk, blk), blk)], snd_sems.at[0], kv_sems.at[i],
                   ring.sibling()).wait_recv()
            forward(i, c).start()
    for i in range(num_tx * n_chip // 2):
        remote(st.at[0, 0, 0], qh_hbm.at[pl.ds(i * blk, blk)], snd_sems.at[0], q_sems.at[i], ring.sibling()).wait_recv()
    for i in range(num_tx * n_chip):
        forward(i, 1 - c).wait_recv()
        forward(i, c).wait_send()
    for k in range(n_chip):
        for p in pieces(k):
            sent(*p)
    gather.finish()


def qkv_call(num_tx, num_ty, hid, g1, b1, wq, wk, wv, bq, bk, bv, cos2, sin2, head_w, cid):
    rows, width = hid.shape
    n_chip = num_ty // 2
    loc_w = wq.shape[1]
    loc_heads = loc_w // head_w
    blk = 2 * rows
    n_blk = num_tx * n_chip
    vm = pl.BlockSpec(memory_space=pltpu.VMEM)
    hb = pl.BlockSpec(memory_space=pl.ANY)
    dma = pltpu.SemaphoreType.DMA
    cache = jax.ShapeDtypeStruct((n_chip * blk, loc_w), BF16)
    return pl.pallas_call(
        functools.partial(qkv_kernel, num_tx, num_ty),
        out_shape=(cache, cache, jax.ShapeDtypeStruct((2, n_blk * blk, head_w), BF16),
                   jax.ShapeDtypeStruct((n_blk // 2 * blk, head_w), BF16)),
        in_specs=[vm] * 3 + [hb] * 3 + [vm] * 5,
        out_specs=(vm, vm, hb, hb),
        scratch_shapes=[pltpu.VMEM((width, 3 * loc_w), BF16), pltpu.VMEM((n_chip, blk, width), BF16),
                        pltpu.VMEM((n_chip, loc_heads, 3, blk, head_w), BF16),
                        dma((3,)), dma((2, AG_SEMS)), dma((n_chip * loc_heads * 3,)), dma((n_blk,)), dma((n_blk // 2,)),
                        dma((2, n_blk))],
        compiler_params=pltpu.CompilerParams(collective_id=cid, has_side_effects=True, vmem_limit_bytes=40 << 20),
        cost_estimate=pl.CostEstimate(flops=30_000_000_000, bytes_accessed=8 << 20, transcendentals=0),
        name="qkv",
    )(hid, g1, b1, wq, wk, wv, bq, bk, bv, cos2, sin2)


def attn_kernel(bounds, q_ref, k_ref, v_ref, start_ref, o_ref, s_ref):
    bq, head_dim = q_ref.shape
    n_blocks = pl.num_programs(0)
    blk = pl.program_id(0)
    q0 = (2 * blk + bounds[0]) * bq
    s_min = bounds[1 + blk]
    s_max = bounds[1 + n_blocks + blk]
    lo = s_min // BK
    hi = (q0 + bq - 1) // BK + 1
    diag = q0 // BK
    mid = jnp.minimum((s_max + BK - 1) // BK, diag)
    scale = head_dim ** -0.5 * LOG2E
    q = q_ref[...]
    start = start_ref[...]
    q_pos = q0 + lax.broadcasted_iota(jnp.int32, (bq, BK), 0)

    def fold(op, m, s):
        for i in range(BK // 128):
            m = op(m, s[:, i * 128:(i + 1) * 128])
        return m

    def score(j):
        k = k_ref[0, pl.ds(pl.multiple_of(j * BK, BK), BK), :]
        return lax.dot_general(q, k, (((1,), (1,)), ((), ())), preferred_element_type=F32) * scale

    def masked(j, m):
        s = score(j)
        k_pos = j * BK + lax.broadcasted_iota(jnp.int32, (bq, BK), 1)
        s = jnp.where((k_pos <= q_pos) & (k_pos >= start), s, -1e30)
        s_ref[j] = s
        return fold(jnp.maximum, m, s)

    def plain(j, m):
        s = score(j)
        s_ref[j] = s
        return fold(jnp.maximum, m, s)

    m = jnp.full((bq, 128), -1e30, F32)
    m = lax.fori_loop(lo, mid, masked, m)
    m = lax.fori_loop(mid, diag, plain, m)
    m = lax.fori_loop(diag, hi, masked, m)
    m = jnp.max(m, axis=1, keepdims=True)

    def expo(j, l):
        p = jnp.exp2(s_ref[j] - m)
        s_ref[j] = p
        return fold(jnp.add, l, p)

    l = lax.fori_loop(lo, hi, expo, jnp.zeros((bq, 128), F32))
    inv = 1.0 / jnp.sum(l, axis=1, keepdims=True)

    def apply(j, acc):
        p = (s_ref[j] * inv).astype(BF16)
        v = v_ref[0, pl.ds(pl.multiple_of(j * BK, BK), BK), :]
        return acc + jnp.dot(p, v, preferred_element_type=F32)

    o_ref[...] = lax.fori_loop(lo, hi, apply, jnp.zeros((bq, head_dim), F32)).astype(BF16)


def attention(q, kv, bounds, start, bq):
    n_query, head_dim = q.shape
    n_key = kv.shape[1]
    return pl.pallas_call(
        attn_kernel,
        grid_spec=pltpu.PrefetchScalarGridSpec(
            num_scalar_prefetch=1,
            grid=(n_query // bq,),
            in_specs=[pl.BlockSpec((bq, head_dim), lambda i, b: (i, 0)),
                      pl.BlockSpec((1, n_key, head_dim), lambda i, b: (0, 0, 0)),
                      pl.BlockSpec((1, n_key, head_dim), lambda i, b: (1, 0, 0)),
                      pl.BlockSpec((bq, 1), lambda i, b: (i, 0))],
            out_specs=pl.BlockSpec((bq, head_dim), lambda i, b: (i, 0)),
            scratch_shapes=[pltpu.VMEM((n_key // BK, bq, BK), F32)]),
        out_shape=jax.ShapeDtypeStruct((n_query, head_dim), BF16),
        cost_estimate=pl.CostEstimate(flops=10_000_000_000, bytes_accessed=4 * n_key * head_dim, transcendentals=0),
        name="attn",
    )(bounds, q, kv, kv, start)


def solution(mesh):
    num_tx = mesh.shape['tx']
    num_ty = mesh.shape['ty']
    width_spec = P('dp', ('tx', 'ty'))
    vec_spec = P(None, ('tx', 'ty'))
    proj_spec = P(None, 'tx', 'ty', None)
    head_spec = P(None, 'ty', None)
    cache_spec = P(None, ('dp', 'tx'), 'ty', None)
    in_specs = (width_spec, P('dp'), P('dp'), vec_spec, vec_spec, proj_spec, head_spec, proj_spec, head_spec,
                proj_spec, head_spec, P(None, 'ty', None, 'tx'), vec_spec, vec_spec, vec_spec,
                P(None, 'tx', 'ty'), P(None, ('ty', 'tx')), P(None, 'ty', 'tx'), vec_spec)
    out_specs = (width_spec, cache_spec, cache_spec)

    def device_fn(x_loc, seg_all, pos_all, ln1_gain, ln1_bias, w_q, b_q, w_k, b_k, w_v, b_v, w_o, b_o,
                  ln2_gain, ln2_bias, w_up, b_up, w_down, b_down):
        n_tok = x_loc.shape[0]
        tok_loc = n_tok // num_tx
        L, d_rows, loc_heads, head_dim = w_q.shape
        both = ('tx', 'ty')
        blk = 2 * tok_loc // num_ty
        core = lax.axis_index('ty') % 2

        q_start = lax.axis_index('tx') * tok_loc
        pos_q = lax.dynamic_slice_in_dim(pos_all, q_start, tok_loc, 0)
        inv_freq = jnp.exp(jnp.arange(head_dim // 2, dtype=F32) * (-2.0 * math.log(ROPE_THETA) / head_dim))
        angles = pos_q.astype(F32)[:, None] * inv_freq[None, :]
        cos_t, sin_t = jnp.cos(angles), jnp.sin(angles)
        cos2 = jnp.concatenate([cos_t, cos_t], axis=1)
        sin2 = jnp.concatenate([-sin_t, sin_t], axis=1)
        start = (jnp.arange(n_tok, dtype=jnp.int32) - pos_all).reshape(-1, 2, blk)
        start = lax.dynamic_index_in_dim(start, core, 1, keepdims=False)
        bounds = jnp.concatenate([core[None].astype(jnp.int32), start[:, 0], start[:, -1]])
        start = start.reshape(-1, 1)

        def gathered(l):
            wq, wk, wv = [lax.all_gather(w[l].reshape(d_rows, -1), 'tx', axis=0, tiled=True) for w in (w_q, w_k, w_v)]
            wo = lax.all_gather(w_o[l].reshape(-1, w_o.shape[-1]), 'tx', axis=0, tiled=False)
            wo = lax.all_gather(wo, 'ty', axis=1, tiled=True)
            wu = lax.all_gather(w_up[l], 'tx', axis=0, tiled=True)
            wd = lax.all_gather(w_down[l], 'tx', axis=0, tiled=False)
            return wq, wk, wv, wo, wu, wd

        weights = [gathered(l) for l in range(L)]
        hidden = lax.all_to_all(x_loc, both, split_axis=0, concat_axis=1, tiled=True)
        vecs = jnp.concatenate([ln1_gain, ln1_bias, ln2_gain, ln2_bias, b_o, b_down], axis=0)
        vecs = lax.all_gather(vecs, both, axis=1, tiled=True)
        b_up_all = lax.all_gather(b_up, 'tx', axis=1, tiled=True)
        k_list = []
        v_list = []
        for l in range(L):
            wq, wk, wv, wo, wu, wd = weights[l]
            vec = [vecs[i * L + l][None] for i in range(6)]
            k, v, kv, q = qkv_call(num_tx, num_ty, hidden, vec[0], vec[1], wq, wk, wv, b_q[l].reshape(1, -1),
                                   b_k[l].reshape(1, -1), b_v[l].reshape(1, -1), cos2, sin2, head_dim, 1)
            o = attention(q, kv, bounds, start, blk)
            hidden = mlp_call(num_tx, num_ty, o, hidden, wo, wu, wd, vec[4], vec[2], vec[3], b_up_all[l][None], vec[5], 2)
            k_list.append(k.reshape(tok_loc, loc_heads, head_dim))
            v_list.append(v.reshape(tok_loc, loc_heads, head_dim))
        y = lax.all_to_all(hidden, both, split_axis=1, concat_axis=0, tiled=True)
        return y, jnp.stack(k_list), jnp.stack(v_list)

    return jax.shard_map(device_fn, mesh=mesh, in_specs=in_specs, out_specs=out_specs, check_vma=False)
```

time: 1630 us -> 643 us (0.39)
  waiting for transfers between devices: 1160 us -> 206 us
  Pallas kernels: 0 us -> 315 us
  matrix products: 157 us -> 0 us
  blocking collectives: 187 us -> 37.3 us
  other arithmetic: 66.8 us -> 8.98 us
    reduce_scatter x12 -> x0, waiting for transfers between devices: 715 us -> none  [the longest x2 289 us: device_fn(): up_sum = lax.psum_scatter(up_part, 'tx', scatter_dimension=1, tiled=True)]
    pallas_call x0 -> x6, Pallas kernels: none -> 315 us  [the longest x2 166 us: mlp_call(): pl.pallas_call(functools.partial(mlp_kernel, num_tx, num_ty), out_shape=j...]
    all_gather x12 -> x14, waiting for transfers between devices: 443 us -> 199 us  [the longest x2 98.9 us: gathered(): wo = lax.all_gather(wo, 'ty', axis=1, tiled=True)]
    psum x4 -> x0, blocking collectives: 187 us -> none  [norm_sharded(): norm_sums = lax.psum(local_sums, ('tx', 'ty'))]
    dot_general x44 -> x0, matrix products: 157 us -> none  [the longest x16 45.7 us: one_block(): jnp.einsum('qkgd,skd->kgqs', q_blk, k_blk, preferred_element_type=jnp.flo...]
    all_gather x0 -> x2, blocking collectives: none -> 37.3 us  [the longest x1 30.1 us: device_fn(): vecs = lax.all_gather(vecs, both, axis=1, tiled=True)]
    convert_element_type x10 -> x1, other arithmetic: 22 us -> 0.01 us  [device_fn(): angles = pos_q.astype(F32)[:, None] * inv_freq[None, :]]
    reduce_sum x20 -> x0, other arithmetic: 17.3 us -> none  [the longest x16 11.5 us: one_block(): attn_prob = jax.nn.softmax(scores, axis=-1).astype(jnp.bfloat16)]
  transfers between devices with their start and end apart: 24 -> 16, of which waited for: 24 -> 8; matrix products, arithmetic and copies ran while one was open for 3% -> 5% of each run, Pallas kernels for 0% -> 37%
where the time goes in v1:
time: 643 us; the launch traced here: 634 us
  Pallas kernels  315 us (49%)
  waiting for transfers between devices  206 us (32%)
  local copies, waits for them, and re-layouts  37.3 us (6%)
  blocking collectives  37.3 us (6%)
  starting transfers between devices  15 us (2%)
  between operations  14.8 us (2%)
  other arithmetic  8.98 us (1%)
    pallas_call x2, Pallas kernels, mlp_call(): pl.pallas_call(functools.partial(mlp_kernel, num_tx, num_ty), out_shape=j...  166 us
    all_gather x2, waiting for transfers between devices, gathered(): wo = lax.all_gather(wo, 'ty', axis=1, tiled=True)  98.9 us
    pallas_call x2, Pallas kernels, qkv_call(): pl.pallas_call(functools.partial(qkv_kernel, num_tx, num_ty), out_shape=(...  97.3 us
    pallas_call x2, Pallas kernels, attention(): pl.pallas_call(attn_kernel, grid_spec=pltpu.PrefetchScalarGridSpec(num_sc...  51.1 us
    all_gather x2, waiting for transfers between devices, gathered(): wu = lax.all_gather(w_up[l], 'tx', axis=0, tiled=True)  48.1 us
    all_gather x6, waiting for transfers between devices, gathered(): lax.all_gather(w[l].reshape(d_rows, -1), 'tx', axis=0, tiled=True)  40.8 us
    all_gather x1, blocking collectives, device_fn(): vecs = lax.all_gather(vecs, both, axis=1, tiled=True)  30.1 us
    unnamed x65, local copies, waits for them, and re-layouts  17.3 us
  transfers between devices with their start and end apart: 16, of which 8 were waited for; matrix products, arithmetic and copies ran while one was open for 5% of the time, Pallas kernels for 37%

profile of v1, /device:TPU:97, one launch (start us, length us, event | category | flops | bytes accessed | tf_op | source)
XLA Modules:
  0.0 633.5 jit_solution(7275512235198607652)
XLA Ops:
  7.3 2.0 fusion.3
  18.7 3.0 fusion.2
  21.8 11.5 %all-gather.24.cloned.1.call-done = bf16[4,256,512]{2,1,0:T(8,128)(2,1)} async-done(((bf16[1,256,512]{2,1,0:T(8,128)(2,1)}), bf16[4,256,512]{2,1,0:T(8,128)(2,1)}) %all-gather.24.cloned.1.call-update) | async-done | bytes 1048592 | tf_op jit(solution)/shard_map/all_gather | solution.py:602
  38.5 7.9 %all-to-all-start = ((bf16[32,128,64]{1,2,0:T(8,128)(2,1)}), bf16[32,128,64]{1,2,0:T(8,128)(2,1)}, u32[]{:S(2)}, u32[]{:S(2)}) async-start(bf16[32,128,64]{1,2,0:T(8,128)(2,1)} %copy_bitcast_fusion.1), calls=%async_computation | async-start | bytes 1048576 | tf_op jit(solution)/shard_map/all_to_all | solution.py:609
  48.0 30.1 %all-gather.2 = bf16[32,64,12]{1,2,0:T(8,128)(2,1)S(1)} all-gather(bf16[1,64,12]{1,2,0:T(8,128)(2,1)S(1)} %bitcast.105), channel_id=1, replica_groups=mesh['dp'=1,'tx'=4,'ty'=8] {'tx','ty'}, dimensions={0}, use_global_device_ids=true | all-gather | bytes 50688 | tf_op jit(solution)/shard_map/all_gather | solution.py:611
  78.3 7.2 %all_gather.56 = bf16[2,1024]{1,0:T(2,128)(2,1)S(1)} all-gather(bf16[2,256]{1,0:T(2,128)(2,1)S(1)} %copy-done.16), channel_id=1, replica_groups=mesh['dp'=1,'tx'=4,'ty'=8] {'tx'}, dimensions={1}, use_global_device_ids=true | all-gather | bytes 5120 | tf_op jit(solution)/shard_map/all_gather | solution.py:612
  85.7 1.9 fusion
  91.4 17.4 %all-gather.20.cloned.1.call-done.wk_hbm = bf16[2048,256]{1,0:T(8,128)(2,1)} async-done(((bf16[512,256]{1,0:T(8,128)(2,1)}), bf16[2048,256]{1,0:T(8,128)(2,1)}) %all-gather.20.cloned.1.call-update) | async-done | bytes 1048592 | tf_op jit(solution)/shard_map/all_gather | solution.py:601
  108.8 23.3 %all-gather.22.cloned.1.call-done.wv_hbm = bf16[2048,256]{1,0:T(8,128)(2,1)} async-done(((bf16[512,256]{1,0:T(8,128)(2,1)}), bf16[2048,256]{1,0:T(8,128)(2,1)}) %all-gather.22.cloned.1.call-update) | async-done | bytes 1048592 | tf_op jit(solution)/shard_map/all_gather | solution.py:601
  135.7 50.1 %qkv.2 = (bf16[1024,256]{1,0:T(8,128)(2,1)S(1)}, bf16[1024,256]{1,0:T(8,128)(2,1)S(1)}, bf16[2,4096,128]{2,1,0:T(8,128)(2,1)S(1)}, bf16[2048,128]{1,0:T(8,128)(2,1)S(1)}) custom-call(bf16[128,2048]{1,0:T(8,128)(2,1)S(1)} %copy.49.hid_ref, bf16[1,2048]{1,0:T(2,128)(2,1)S(1)} %get-tuple-element.44.g1_ref, bf16[1,2048]{1,0:T(2,128)(2,1)S(1)} %get-tuple-element.43.b1_ref, ...), custom_call_target="tpu_custom_call" | custom-call | flops 30000001024 | bytes 8388608 | tf_op jit(solution)/shard_map/qkv/pallas_call | solution.py:471
  187.9 25.6 %attn.2.o_hbm = bf16[2048,128]{1,0:T(8,128)(2,1)} custom-call(s32[17]{0:T(128)} %pad_add_fusion.bounds, bf16[2048,128]{1,0:T(8,128)(2,1)} %copy-done.12, bf16[2,4096,128]{2,1,0:T(8,128)(2,1)} %copy-done.10, bf16[2,4096,128]{2,1,0:T(8,128)(2,1)} %copy-done.10, s32[2048,1]{1,0:T(8,128)} %copy.50.start_ref), custom_call_target="tpu_custom_call" | custom-call | flops 10000000000 | bytes 2097152 | tf_op jit(solution)/shard_map/attn/pallas_call | solution.py:549
  213.5 29.7 %all-gather.42.cloned.1.call-done = bf16[1,2048,1024]{2,1,0:T(8,128)(2,1)} async-done(((bf16[1,512,1024]{2,1,0:T(8,128)(2,1)}), bf16[1,2048,1024]{2,1,0:T(8,128)(2,1)}) %all-gather.42.cloned.1.call-update) | async-done | bytes 4194320 | tf_op jit(solution)/shard_map/all_gather | solution.py:604
  243.2 49.5 %all-gather.26.cloned.1.call-done.wo_hbm = bf16[4,2048,512]{2,1,0:T(8,128)(2,1)} async-done(((bf16[4,256,512]{2,1,0:T(8,128)(2,1)}), bf16[4,2048,512]{2,1,0:T(8,128)(2,1)}) %all-gather.26.cloned.1.call-update) | async-done | bytes 8388624 | tf_op jit(solution)/shard_map/all_gather | solution.py:603
  292.7 83.2 %mlp.2.hid_ref = bf16[128,2048]{1,0:T(8,128)(2,1)} custom-call(bf16[2048,128]{1,0:T(8,128)(2,1)} %attn.2.o_hbm, bf16[128,2048]{1,0:T(8,128)(2,1)} %copy-done.2, bf16[4,2048,512]{2,1,0:T(8,128)(2,1)} %all-gather.26.cloned.1.call-done.wo_hbm, bf16[2048,1024]{1,0:T(8,128)(2,1)} %bitcast.106, bf16[4,1024,512]{2,1,0:T(8,128)(2,1)} %all-gather.28.cloned.1.call-done.wd_hbm, ...), custom_call_target="tpu_custom_call" | custom-call | flops 80000000000 | bytes 20971520 | tf_op jit(solution)/shard_map/mlp/pallas_call | solution.py:327
  380.7 47.3 %qkv.3 = (bf16[1024,256]{1,0:T(8,128)(2,1)S(1)}, bf16[1024,256]{1,0:T(8,128)(2,1)S(1)}, bf16[2,4096,128]{2,1,0:T(8,128)(2,1)S(1)}, bf16[2048,128]{1,0:T(8,128)(2,1)S(1)}) custom-call(bf16[128,2048]{1,0:T(8,128)(2,1)S(1)} %copy-done.13, bf16[1,2048]{1,0:T(2,128)(2,1)S(1)} %get-tuple-element.38.g1_ref, bf16[1,2048]{1,0:T(2,128)(2,1)S(1)} %get-tuple-element.37.b1_ref, ...), custom_call_target="tpu_custom_call" | custom-call | flops 30000001024 | bytes 8388608 | tf_op jit(solution)/shard_map/qkv/pallas_call | solution.py:471
  430.0 25.6 %attn.3.o_hbm = bf16[2048,128]{1,0:T(8,128)(2,1)} custom-call(s32[17]{0:T(128)} %pad_add_fusion.bounds, bf16[2048,128]{1,0:T(8,128)(2,1)} %copy-done.11, bf16[2,4096,128]{2,1,0:T(8,128)(2,1)} %copy-done.9, bf16[2,4096,128]{2,1,0:T(8,128)(2,1)} %copy-done.9, s32[2048,1]{1,0:T(8,128)} %copy.50.start_ref), custom_call_target="tpu_custom_call" | custom-call | flops 10000000000 | bytes 2097152 | tf_op jit(solution)/shard_map/attn/pallas_call | solution.py:549
  455.6 18.3 %all-gather.44.cloned.1.call-done = bf16[1,2048,1024]{2,1,0:T(8,128)(2,1)} async-done(((bf16[1,512,1024]{2,1,0:T(8,128)(2,1)}), bf16[1,2048,1024]{2,1,0:T(8,128)(2,1)}) %all-gather.44.cloned.1.call-update) | async-done | bytes 4194320 | tf_op jit(solution)/shard_map/all_gather | solution.py:604
  473.9 49.4 %all-gather.38.cloned.1.call-done.wo_hbm = bf16[4,2048,512]{2,1,0:T(8,128)(2,1)} async-done(((bf16[4,256,512]{2,1,0:T(8,128)(2,1)}), bf16[4,2048,512]{2,1,0:T(8,128)(2,1)}) %all-gather.38.cloned.1.call-update) | async-done | bytes 8388624 | tf_op jit(solution)/shard_map/all_gather | solution.py:603
  523.4 82.9 %mlp.3 = bf16[128,2048]{1,0:T(8,128)(2,1)} custom-call(bf16[2048,128]{1,0:T(8,128)(2,1)} %attn.3.o_hbm, bf16[128,2048]{1,0:T(8,128)(2,1)} %mlp.2.hid_ref, bf16[4,2048,512]{2,1,0:T(8,128)(2,1)} %all-gather.38.cloned.1.call-done.wo_hbm, bf16[2048,1024]{1,0:T(8,128)(2,1)} %bitcast.107, bf16[4,1024,512]{2,1,0:T(8,128)(2,1)} %all-gather.40.cloned.1.call-done.wd_hbm, ...), custom_call_target="tpu_custom_call" | custom-call | flops 80000000000 | bytes 20971520 | tf_op jit(solution)/shard_map/mlp/pallas_call | solution.py:327
  606.3 2.0 copy.53
  608.3 6.3 all-to-all-start.1
  615.9 3.6 pad_maximum_fusion.1
  619.5 2.5 pad_maximum_fusion
  622.0 3.7 all-to-all-done.1
  (127 shorter events, 34.8 us)
Async XLA Ops:
  7.2 30.3 %copy-start = (bf16[4096,64]{0,1:T(8,128)(2,1)S(1)}, bf16[4096,64]{0,1:T(8,128)(2,1)}, u32[]{:S(2)}) copy-start(bf16[4096,64]{0,1:T(8,128)(2,1)} %param.19) | copy-start | bytes 1572868
  7.2 26.1 %all-gather.24.cloned.1.call-start = ((), (), s32[]{:S(2)}) async-start(), calls=%async_computation.5 | async-start | bytes 1310720 | tf_op jit(solution)/shard_map/all_gather | solution.py:602
  9.3 81.9 %all-gather.36.cloned.1.call-start = ((), (), s32[]{:S(2)}) async-start(), calls=%async_computation.11 | async-start | bytes 1310720 | tf_op jit(solution)/shard_map/all_gather | solution.py:602
  10.2 81.2 %all-gather.18.cloned.1.call-start = ((), (), s32[]{:S(2)}) async-start(), calls=%async_computation.2 | async-start | bytes 1310720 | tf_op jit(solution)/shard_map/all_gather | solution.py:601
  12.4 96.3 %all-gather.20.cloned.1.call-start = ((), (), s32[]{:S(2)}) async-start(), calls=%async_computation.3 | async-start | bytes 1310720 | tf_op jit(solution)/shard_map/all_gather | solution.py:601
  14.7 117.4 %all-gather.22.cloned.1.call-start = ((), (), s32[]{:S(2)}) async-start(), calls=%async_computation.4 | async-start | bytes 1310720 | tf_op jit(solution)/shard_map/all_gather | solution.py:601
  17.0 196.5 %all-gather.28.cloned.1.call-start = ((), (), s32[]{:S(2)}) async-start(), calls=%async_computation.7 | async-start | bytes 5242880 | tf_op jit(solution)/shard_map/all_gather | solution.py:605
  18.6 224.6 %all-gather.42.cloned.1.call-start = ((), (), s32[]{:S(2)}) async-start(), calls=%async_computation.14 | async-start | bytes 5242880 | tf_op jit(solution)/shard_map/all_gather | solution.py:604
  21.7 24.8 %copy-start.15 = (s32[4096]{0:T(1024)S(1)}, s32[4096]{0:T(1024)}, u32[]{:S(2)}) copy-start(s32[4096]{0:T(1024)} %param.20) | copy-start | bytes 49156
  21.7 270.9 %all-gather.26.cloned.1.call-start = ((), (), s32[]{:S(2)}) async-start(), calls=%async_computation.6 | async-start | bytes 9437184 | tf_op jit(solution)/shard_map/all_gather | solution.py:603
  33.3 14.5 %copy-start.25 = (bf16[2,64]{1,0:T(2,128)(2,1)S(1)}, bf16[2,64]{1,0:T(2,128)(2,1)}, u32[]{:S(2)}) copy-start(bf16[2,64]{1,0:T(2,128)(2,1)} %param.36) | copy-start | bytes 772
  33.4 44.8 %copy-start.17 = (bf16[2,2,128]{2,1,0:T(2,128)(2,1)S(1)}, bf16[2,2,128]{2,1,0:T(2,128)(2,1)}, u32[]{:S(2)}) copy-start(bf16[2,2,128]{2,1,0:T(2,128)(2,1)} %param.24) | copy-start | bytes 3076
  33.4 44.9 %copy-start.16 = (bf16[2,256]{1,0:T(2,128)(2,1)S(1)}, bf16[2,256]{1,0:T(2,128)(2,1)}, u32[]{:S(2)}) copy-start(bf16[2,256]{1,0:T(2,128)(2,1)} %param.34) | copy-start | bytes 3076
  33.4 342.4 %all-gather.30.cloned.1.call-start = ((), (), s32[]{:S(2)}) async-start(), calls=%async_computation.8 | async-start | bytes 1310720 | tf_op jit(solution)/shard_map/all_gather | solution.py:601
  34.3 341.6 %all-gather.32.cloned.1.call-start = ((), (), s32[]{:S(2)}) async-start(), calls=%async_computation.9 | async-start | bytes 1310720 | tf_op jit(solution)/shard_map/all_gather | solution.py:601
  35.2 340.7 %all-gather.34.cloned.1.call-start = ((), (), s32[]{:S(2)}) async-start(), calls=%async_computation.10 | async-start | bytes 1310720 | tf_op jit(solution)/shard_map/all_gather | solution.py:601
  36.1 419.5 %all-gather.40.cloned.1.call-start = ((), (), s32[]{:S(2)}) async-start(), calls=%async_computation.13 | async-start | bytes 5242880 | tf_op jit(solution)/shard_map/all_gather | solution.py:605
  36.7 437.2 %all-gather.44.cloned.1.call-start = ((), (), s32[]{:S(2)}) async-start(), calls=%async_computation.15 | async-start | bytes 5242880 | tf_op jit(solution)/shard_map/all_gather | solution.py:604
  37.5 50.4 %copy-start.18 = (bf16[2,2,128]{2,1,0:T(2,128)(2,1)S(1)}, bf16[2,2,128]{2,1,0:T(2,128)(2,1)}, u32[]{:S(2)}) copy-start(bf16[2,2,128]{2,1,0:T(2,128)(2,1)} %param.28) | copy-start | bytes 3076
  37.5 50.4 %copy-start.19 = (bf16[2,2,128]{2,1,0:T(2,128)(2,1)S(1)}, bf16[2,2,128]{2,1,0:T(2,128)(2,1)}, u32[]{:S(2)}) copy-start(bf16[2,2,128]{2,1,0:T(2,128)(2,1)} %param.26) | copy-start | bytes 3076
  38.5 51.5 %all-to-all-start = ((bf16[32,128,64]{1,2,0:T(8,128)(2,1)}), bf16[32,128,64]{1,2,0:T(8,128)(2,1)}, u32[]{:S(2)}, u32[]{:S(2)}) async-start(bf16[32,128,64]{1,2,0:T(8,128)(2,1)} %copy_bitcast_fusion.1), calls=%async_computation | async-start | bytes 1048576 | tf_op jit(solution)/shard_map/all_to_all | solution.py:609
  46.4 477.0 %all-gather.38.cloned.1.call-start = ((), (), s32[]{:S(2)}) async-start(), calls=%async_computation.12 | async-start | bytes 9437184 | tf_op jit(solution)/shard_map/all_gather | solution.py:603
  91.2 94.6 %copy-start.2 = (bf16[128,2048]{1,0:T(8,128)(2,1)}, bf16[128,2048]{1,0:T(8,128)(2,1)S(1)}, u32[]{:S(2)}) copy-start(bf16[128,2048]{1,0:T(8,128)(2,1)S(1)} %copy.49.hid_ref) | copy-start | bytes 1572868
  608.3 17.3 %all-to-all-start.1 = ((bf16[128,32,64]{0,2,1:T(8,128)(2,1)}), bf16[128,32,64]{0,2,1:T(8,128)(2,1)S(1)}, u32[]{:S(2)}, u32[]{:S(2)}) async-start(bf16[128,32,64]{0,2,1:T(8,128)(2,1)} %bitcast.11), calls=%async_computation.1 | async-start | bytes 1048576 | tf_op jit(solution)/shard_map/all_to_all | solution.py:624
  (18 other events, 106.1 us)
Sparse Core Ops, SparseCore 0:
  10.2 23.1 all-gather.23
  34.9 26.9 all-gather.35
  63.4 22.1 all-gather.17
  87.0 21.6 all-gather.19
  110.2 21.8 all-gather.21
  133.5 62.8 all-gather.27
  197.9 45.2 all-gather.41
  244.8 47.8 all-gather.25
  294.2 21.7 all-gather.29
  317.5 19.5 all-gather.31
  338.7 21.8 all-gather.33
  361.9 61.1 all-gather.39
  425.2 48.6 all-gather.43
  475.4 47.9 all-gather.37
